TPU v7x, 32 devices: a whole 2x2x4 slice. The times are simulated.
32 devices in a mesh: dp: 8 (over z, y), mp: 4 (over x, core).
Axes of the slice: x: 2, y: 2, z: 4, core: 2. Of those that a mesh axis runs over, the one named last changes fastest.
Arguments:
- noise_blocks: bfloat16 [64, 12800], P('dp'), may hold values from -6 to 6
- data_blocks: bfloat16 [64, 12800], P('dp'), may hold values from -6 to 6
- destination: int32 [64], replicated, may hold values from 0 to 63, as said below
- utt_blocks: int32 [8, 4], P('dp'), may hold values from 1 to 4, 8 in all within a row
- span_start: int32 [8, 4], P('dp'), may hold values from 0 to 19
- span_size: int32 [8, 4], P('dp'), may hold values from 44 to 64
- timestep: int32 [8, 4], P('dp'), may hold values from 1 to 63
- in_weight: bfloat16 [200, 1024], replicated, may hold values from -0.4375 to 0.4375
- norm_gain: bfloat16 [1024], replicated, may hold values from 0.5 to 1.5
- qkv_weight: bfloat16 [1024, 3, 512], P(None, None, 'mp'), may hold values from -4 to 4
- out_proj: bfloat16 [512, 1024], P('mp'), may hold values from -0.25 to 0.25
- final_gain: bfloat16 [1024], replicated, may hold values from 0.25 to 1.75
- vel_weight: bfloat16 [1024, 100], replicated, may hold values from -0.1875 to 0.1875
Outputs:
- grad_qkv: float32 [1024, 3, 512], P('dp', None, 'mp')
- grad_out: float32 [512, 1024], P('mp', 'dp')
Inputs may be any that keep to these rules, and one draw needn't show every extreme that they name: `destination`: A permutation of the 64 bin positions; a device sends to each bin either none or exactly 1 of its blocks.
All inputs are finite; a program needn't handle non-finite values.
Results may differ from a plain program's by a relative error of at most 0.004.
Values may be sent and summed in bfloat16 or wider, within the bound.
A program may use at most 64 MiB of HBM per device.

v0:
```python
import jax
import jax.numpy as jnp
from jax import lax
from jax.sharding import PartitionSpec as P

HEAD_DIM = 64
BLOCK = 128


def frame_table(lengths, starts, sizes, steps, rows):
    ends = jnp.cumsum(lengths)
    frame = jnp.arange(rows, dtype=jnp.int32)
    block_index = frame // BLOCK
    segment = jnp.sum((block_index[:, None] >= ends[None, :]).astype(jnp.int32), axis=1)
    member = segment[:, None] == jnp.arange(lengths.shape[0], dtype=jnp.int32)[None, :]
    first = jnp.sum(jnp.where(member, (ends - lengths)[None, :], 0), axis=1) * BLOCK
    span = jnp.sum(jnp.where(member, lengths[None, :], 0), axis=1) * BLOCK
    lower = jnp.sum(jnp.where(member, starts[None, :], 0), axis=1)
    upper = lower + jnp.sum(jnp.where(member, sizes[None, :], 0), axis=1)
    inside = 64 * (frame - first)
    masked = ((inside >= lower * span) & (inside < upper * span)).astype(jnp.float32)
    level = jnp.sum(jnp.where(member, steps[None, :], 0), axis=1).astype(jnp.float32) / 64.0
    return (segment, masked, level)


def attend(query, keys, values, segment):
    rows, width = query.shape
    heads = width // HEAD_DIM
    block = min(512, rows)
    reach = min(4, rows // BLOCK // 2) * BLOCK
    window = min(rows, block + 2 * reach)
    blocks = rows // block
    query_blocks = query.reshape(blocks, block, heads, HEAD_DIM)
    segment_blocks = segment.reshape(blocks, block)
    firsts = jnp.clip(jnp.arange(blocks, dtype=jnp.int32) * block - reach, 0, rows - window)
    keyed = keys.reshape(rows, heads, HEAD_DIM)
    valued = values.reshape(rows, heads, HEAD_DIM)

    def one_block(item):
        query_block, segment_block, first = item
        scores = jnp.einsum(
            "qhd,khd->hqk", query_block, keyed, preferred_element_type=jnp.float32
        ) * HEAD_DIM ** (-0.5)
        scores = jnp.where((segment_block[:, None] == segment[None, :])[None], scores, -1e30)
        top = jnp.max(scores, axis=-1, keepdims=True)
        weights = jnp.exp(scores - top)
        probs = (weights / jnp.sum(weights, axis=-1, keepdims=True)).astype(jnp.bfloat16)
        return jnp.einsum(
            "hqk,khd->qhd", probs, valued, preferred_element_type=jnp.float32
        ).reshape(block, width)

    return lax.map(jax.checkpoint(one_block), (query_blocks, segment_blocks, firsts)).reshape(
        rows, width
    )


def shards(
    noise_blocks,
    data_blocks,
    destination,
    utt_blocks,
    span_start,
    span_size,
    timestep,
    in_weight,
    norm_gain,
    qkv_weight,
    out_proj,
    final_gain,
    vel_weight,
):
    sources = lax.axis_size("dp")
    here = lax.axis_index("dp")
    per_dev = noise_blocks.shape[0]
    depth = max(1, per_dev // sources)
    lanes_total = sources * depth
    table = destination.reshape(sources, per_dev)
    owner = table // per_dev
    order = jnp.arange(per_dev, dtype=jnp.int32)
    earlier = (owner[:, :, None] == owner[:, None, :]) & (
        order[None, None, :] < order[None, :, None]
    )
    rank = jnp.sum(earlier.astype(jnp.int32), axis=2)
    code = jnp.arange(sources, dtype=jnp.int32)[:, None] * depth + rank
    mine_owner = lax.dynamic_index_in_dim(owner, here, 0, keepdims=False)
    mine_rank = lax.dynamic_index_in_dim(rank, here, 0, keepdims=False)
    lanes = jnp.arange(lanes_total, dtype=jnp.int32)
    packing = (lanes[:, None] == (mine_owner * depth + mine_rank)[None, :]).astype(jnp.bfloat16)
    wanted = here * per_dev + order
    hit = table[None, :, :] == wanted[:, None, None]
    source_code = jnp.sum(jnp.where(hit, code[None, :, :], 0), axis=(1, 2))
    unpacking = (source_code[:, None] == lanes[None, :]).astype(jnp.bfloat16)

    def outgoing(blocks):
        sent = jnp.dot(packing, blocks, preferred_element_type=jnp.float32).astype(jnp.bfloat16)
        return sent.reshape(sources, depth, blocks.shape[1])

    def incoming(arrived):
        flat = arrived.reshape(lanes_total, arrived.shape[2])
        return jnp.dot(unpacking, flat, preferred_element_type=jnp.float32).astype(jnp.bfloat16)

    got_noise, got_data = (
        lax.all_to_all(outgoing(noise_blocks), "dp", split_axis=0, concat_axis=0, tiled=True),
        lax.all_to_all(outgoing(data_blocks), "dp", split_axis=0, concat_axis=0, tiled=True),
    )
    bin_noise = incoming(got_noise)
    bin_data = incoming(got_data)
    rows = per_dev * BLOCK
    mel = noise_blocks.shape[1] // BLOCK
    noise = bin_noise.reshape(rows, mel).astype(jnp.float32)
    data = bin_data.reshape(rows, mel).astype(jnp.float32)
    segment, masked, level = frame_table(
        utt_blocks[0], span_start[0], span_size[0], timestep[0], rows
    )
    noisy = (1.0 - level[:, None]) * noise + level[:, None] * data
    cond = data * (1.0 - masked[:, None])
    target = data - noise
    inputs = jnp.concatenate([noisy, cond], axis=1).astype(jnp.bfloat16)
    hidden0 = jnp.dot(inputs, in_weight, preferred_element_type=jnp.float32)
    scale = lax.rsqrt(jnp.mean(hidden0 * hidden0, axis=1, keepdims=True) + 1e-06)
    normed = (hidden0 * scale * norm_gain.astype(jnp.float32)[None, :]).astype(jnp.bfloat16)
    query = jnp.dot(normed, qkv_weight[:, 0, :], preferred_element_type=jnp.float32).astype(
        jnp.bfloat16
    )
    keys = jnp.dot(normed, qkv_weight[:, 1, :], preferred_element_type=jnp.float32).astype(
        jnp.bfloat16
    )
    values = jnp.dot(normed, qkv_weight[:, 2, :], preferred_element_type=jnp.float32).astype(
        jnp.bfloat16
    )
    heads_out, pullback = jax.vjp(lambda a, b, c: attend(a, b, c, segment), query, keys, values)
    attended = heads_out.astype(jnp.bfloat16)
    partial_mix = jnp.dot(attended, out_proj, preferred_element_type=jnp.float32)
    mixed = lax.psum(partial_mix.astype(jnp.bfloat16), "mp").astype(jnp.float32)
    hidden1 = (hidden0 + mixed).astype(jnp.bfloat16)
    wide1 = lax.optimization_barrier(hidden1).astype(jnp.float32)
    rscale = lax.rsqrt(jnp.mean(wide1 * wide1, axis=1, keepdims=True) + 1e-06)
    normalized = wide1 * rscale
    gain_out = final_gain.astype(jnp.float32)[None, :]
    final = (normalized * gain_out).astype(jnp.bfloat16)
    velocity = jnp.dot(final, vel_weight, preferred_element_type=jnp.float32)
    count = lax.psum(jnp.sum(masked), "dp")
    error = (2.0 * masked[:, None] * (velocity - target)).astype(jnp.bfloat16)
    grad_final = jnp.dot(error, vel_weight.T, preferred_element_type=jnp.float32)
    scaled = grad_final * gain_out
    back1 = (
        rscale * (scaled - normalized * jnp.mean(scaled * normalized, axis=1, keepdims=True))
    ).astype(jnp.bfloat16)
    back_att = jnp.dot(back1, out_proj.T, preferred_element_type=jnp.float32).astype(jnp.bfloat16)
    dquery, dkeys, dvalues = pullback(back_att.astype(jnp.float32))
    out_terms = jnp.dot(attended.T, back1, preferred_element_type=jnp.float32)
    qkv_terms = jnp.stack(
        [
            jnp.dot(normed.T, dquery, preferred_element_type=jnp.float32),
            jnp.dot(normed.T, dkeys, preferred_element_type=jnp.float32),
            jnp.dot(normed.T, dvalues, preferred_element_type=jnp.float32),
        ],
        axis=1,
    )
    summed_qkv, summed_out = (
        lax.psum_scatter(qkv_terms, "dp", scatter_dimension=0, tiled=True),
        lax.psum_scatter(out_terms, "dp", scatter_dimension=1, tiled=True),
    )
    return (summed_qkv / count, summed_out / count)


def solution(mesh):
    in_specs = (
        P("dp", None),
        P("dp", None),
        P(),
        P("dp", None),
        P("dp", None),
        P("dp", None),
        P("dp", None),
        P(),
        P(),
        P(None, None, "mp"),
        P("mp", None),
        P(),
        P(),
    )
    out_specs = (P("dp", None, "mp"), P("mp", "dp"))
    return jax.shard_map(shards, mesh=mesh, in_specs=in_specs, out_specs=out_specs, check_vma=False)
```

profile of v0, /device:TPU:0, one launch (start us, length us, event | category | flops | bytes accessed | tf_op | source)
XLA Modules:
  0.0 272.0 jit_solution(2920325727797531894)
XLA Ops:
  8.3 1.1 fusion.60
  11.4 7.3 %all-to-all-start = ((bf16[8,2,6400]{2,1,0:T(2,128)(2,1)}), bf16[8,2,6400]{2,1,0:T(2,128)(2,1)S(1)}, u32[]{:S(2)}, u32[]{:S(2)}) async-start(bf16[8,2,6400]{2,1,0:T(2,128)(2,1)} %reshape.344), calls=%async_computation | async-start | bytes 409600 | tf_op jit(solution)/shard_map/all_to_all | solution.py:103
  21.7 1.1 fusion.61
  24.4 2.4 all-to-all-done
  26.8 3.6 %all-to-all-start.1 = ((bf16[8,2,6400]{2,1,0:T(2,128)(2,1)}), bf16[8,2,6400]{2,1,0:T(2,128)(2,1)S(1)}, u32[]{:S(2)}, u32[]{:S(2)}) async-start(bf16[8,2,6400]{2,1,0:T(2,128)(2,1)} %reshape.342), calls=%async_computation.1 | async-start | bytes 409600 | tf_op jit(solution)/shard_map/all_to_all | solution.py:104
  33.4 4.8 %all-to-all-done.1 = bf16[8,2,6400]{2,1,0:T(2,128)(2,1)S(1)} async-done(((bf16[8,2,6400]{2,1,0:T(2,128)(2,1)}), bf16[8,2,6400]{2,1,0:T(2,128)(2,1)S(1)}, u32[]{:S(2)}, u32[]{:S(2)}) %all-to-all-start.1) | async-done | bytes 204832 | tf_op jit(solution)/shard_map/all_to_all | solution.py:104
  41.4 1.3 copy-done.16
  44.1 1.2 convolution_convert_fusion.7
  45.5 1.0 copy.56
  46.5 17.6 %while.30 = (s32[]{:T(128)}, bf16[2,512,128]{2,1,0:T(8,128)(2,1)S(1)}, s32[2,512]{1,0:T(2,128)}, s32[1,1024]{1,0:T(1,128)S(1)}, bf16[2,512,2,64]{1,3,2,0:T(8,128...) while((s32[]{:T(128)}, bf16[2,512,128]{2,1,0:T(8,128)(2,1)S(1)}, ...), condition=%wide.region_13.14_spmd, body=%wide.region_10.13_spmd.sunk | while | flops 275252224 | bytes 11815545 | solution.py:52
  47.6 4.5 %fusion.178 = (f32[2,512]{1,0:T(2,128)S(1)}, f32[2,512,1024]{2,1,0:T(8,128)}) fusion(pred[512,1024]{1,0:T(8,128)(4,1)S(1)} %broadcast_compare_fusion.4, bf16[1024,2,64]{0,2,1:T(8,128)(2,1)S(1)} %get-tuple-element.617, bf16[2,512,2,64]{1,3,2,0:T(8,128)(2,1)} %get-tuple-element.616, s32[]{:T(128)} %get-tuple-element.604), kind=kOutput, calls=%fused_computation.176.clone.1 | convolution fusion | flops 138413056 | bytes 5116416 | tf_op jit(solution)/shard_map/jvp()/while/body/eval_jaxpr/sub | solution.py:46
  52.2 3.0 %fusion.179 = bf16[2,512,64]{1,2,0:T(8,128)(2,1)S(1)} fusion(bf16[1024,2,64]{0,2,1:T(8,128)(2,1)S(1)} %copy-done.19, f32[2,512,1024]{2,1,0:T(8,128)} %get-tuple-element.570, f32[2,512]{1,0:T(2,128)S(1)} %get-tuple-element.571), kind=kOutput, calls=%fused_computation.8.clone.1 | convolution fusion | flops 136314880 | bytes 4591616 | tf_op jit(solution)/shard_map/jvp()/while/body/eval_jaxpr/hqk,khd->qhd/dot_general | solution.py:48
  56.4 4.5 %fusion.178 = (f32[2,512]{1,0:T(2,128)S(1)}, f32[2,512,1024]{2,1,0:T(8,128)}) fusion(pred[512,1024]{1,0:T(8,128)(4,1)S(1)} %broadcast_compare_fusion.4, bf16[1024,2,64]{0,2,1:T(8,128)(2,1)S(1)} %get-tuple-element.617, bf16[2,512,2,64]{1,3,2,0:T(8,128)(2,1)} %get-tuple-element.616, s32[]{:T(128)} %get-tuple-element.604), kind=kOutput, calls=%fused_computation.176.clone.1 | convolution fusion | flops 138413056 | bytes 5116416 | tf_op jit(solution)/shard_map/jvp()/while/body/eval_jaxpr/sub | solution.py:46
  60.9 3.0 %fusion.179 = bf16[2,512,64]{1,2,0:T(8,128)(2,1)S(1)} fusion(bf16[1024,2,64]{0,2,1:T(8,128)(2,1)S(1)} %copy-done.19, f32[2,512,1024]{2,1,0:T(8,128)} %get-tuple-element.570, f32[2,512]{1,0:T(2,128)S(1)} %get-tuple-element.571), kind=kOutput, calls=%fused_computation.8.clone.1 | convolution fusion | flops 136314880 | bytes 4591616 | tf_op jit(solution)/shard_map/jvp()/while/body/eval_jaxpr/hqk,khd->qhd/dot_general | solution.py:48
  64.2 2.1 convolution_convert_fusion.5
  66.8 1.0 copy.54
  67.8 48.4 %all-reduce.2.cloned.1.call-done = bf16[1024,1024]{0,1:T(8,128)(2,1)} async-done(((bf16[1024,1024]{0,1:T(8,128)(2,1)}), bf16[1024,1024]{0,1:T(8,128)(2,1)}) %all-reduce.2.cloned.1.call-update) | async-done | bytes 2097168 | tf_op jit(solution)/shard_map/psum | solution.py:134
  116.2 3.6 %add_convert_fusion = bf16[1024,1024]{0,1:T(8,128)(2,1)S(1)} fusion(f32[1024,1024]{0,1:T(8,128)} %copy-done.4, bf16[1024,1024]{0,1:T(8,128)(2,1)} %all-reduce.2.cloned.1.call-done), kind=kLoop, calls=%fused_computation.88 | loop fusion | flops 3145728 | bytes 8388608 | tf_op jit(solution)/shard_map/convert_element_type | solution.py:135
  120.3 4.7 %fusion.66 = (f32[1024]{0:T(1024)S(1)}, f32[1024,1024]{0,1:T(8,128)}) fusion(bf16[1024,1024]{0,1:T(8,128)(2,1)S(1)} %add_convert_fusion, f32[1024]{0:T(1024)S(1)} %convert_element_type.200, f32[1024]{0:T(1024)S(1)} %add_rsqrt_fusion, bf16[1024,100]{0,1:T(8,128)(2,1)} %param.29, f32[1024,100]{0,1:T(8,128)} %copy.54, f32[1024,100]{0,1:T(8,128)S(1)} %copy.55, ...), kind=kOutput, calls=%fused_computation.83 | convolution fusion | flops 429276160 | bytes 7331840 | tf_op jit(solution)/shard_map/dot_general | solution.py:144
  125.0 3.7 %fusion.69 = bf16[1024,1024]{0,1:T(8,128)(2,1)S(1)} fusion(bf16[1024,1024]{0,1:T(8,128)(2,1)} %copy-done.7, f32[1024,1024]{0,1:T(8,128)} %get-tuple-element.459, f32[1024]{0:T(1024)S(1)} %broadcast_multiply_fusion, f32[1024]{0:T(1024)S(1)} %convert_element_type.200, f32[1024]{0:T(1024)S(1)} %add_rsqrt_fusion), kind=kLoop, calls=%fused_computation.86 | loop fusion | flops 7340032 | bytes 8400896 | tf_op jit(solution)/shard_map/convert_element_type | solution.py:148
  128.8 1.6 fusion.126
  132.0 44.7 %while.31 = (s32[]{:T(128)}, bf16[1024,2,64]{0,2,1:T(8,128)(2,1)}, bf16[1024,2,64]{0,2,1:T(8,128)(2,1)}, bf16[2,512,2,64]{1,3,2,0:T(8,128)(2,1)}, bf16[2,512,2,6...) while((s32[]{:T(128)}, bf16[1024,2,64]{0,2,1:T(8,128)(2,1)}, ...), condition=%wide.region_23.24_spmd.clone, body=%wide.region_17.23_spmd.clone.sunk | while | flops 712179712 | bytes 109349352 | solution.py:52
  132.1 1.0 dynamic-slice_bitcast_fusion.2
  133.8 1.0 broadcast_compare_fusion.5
  134.9 2.1 fusion.187
  137.0 1.2 fusion.188
  138.2 2.8 %convert_reduce_fusion.5 = (f32[2,512]{1,0:T(2,128)S(1)}, pred[2,512,1024]{2,1,0:T(32,128)(4,1)S(1)}, f32[2,512]{1,0:T(2,128)S(1)}, bf16[2,512,1024]{2,1,0:T(8,128)(2,1)S(1)}) fusion(f32[2,512]{1,0:T(2,128)S(1)} %get-tuple-element.586, f32[2,512,1024]{2,1,0:T(8,128)S(1)} %get-tuple-element.587, pred[512,1024]{1,0:T(8,128)(4,1)S(1)} %broadcast_compare_fusion.5, ...), kind=kOutput, calls=%fused_computation.30.clone.1 | convolution fusion | flops 144701440 | bytes 8273920 | tf_op jit(solution)/shard_map/transpose(jvp())/while/body/eval_jaxpr/checkpoint/hqk,khd->qhd/dot_general | solution.py:48
  141.0 1.9 fusion.189
  143.0 1.9 copy-done.2
  144.9 2.2 fusion.192
  147.1 4.5 %fusion.191 = bf16[1024,2,64]{0,2,1:T(8,128)(2,1)} fusion(bf16[2,64,512]{2,1,0:T(8,128)(2,1)S(1)} %bitcast.163, f32[2,512]{1,0:T(2,128)} %copy-done.9, f32[2,512,1024]{2,1,0:T(8,128)} %copy-done.1, f32[2,512]{1,0:T(2,128)} %copy-done.11, pred[512,1024]{1,0:T(8,128)(4,1)S(1)} %broadcast_compare_fusion.5, ...), kind=kOutput, calls=%fused_computation.52.clone.1 | convolution fusion | flops 139722752 | bytes 5382145 | tf_op jit(solution)/shard_map/transpose(jvp())/while/body/eval_jaxpr/checkpoint/hqk,khd->qhd/dot_general | solution.py:48
  151.6 2.3 fusion.190
  155.6 1.0 broadcast_compare_fusion.5
  156.7 2.1 fusion.187
  158.8 1.2 fusion.188
  160.0 2.8 %convert_reduce_fusion.5 = (f32[2,512]{1,0:T(2,128)S(1)}, pred[2,512,1024]{2,1,0:T(32,128)(4,1)S(1)}, f32[2,512]{1,0:T(2,128)S(1)}, bf16[2,512,1024]{2,1,0:T(8,128)(2,1)S(1)}) fusion(f32[2,512]{1,0:T(2,128)S(1)} %get-tuple-element.586, f32[2,512,1024]{2,1,0:T(8,128)S(1)} %get-tuple-element.587, pred[512,1024]{1,0:T(8,128)(4,1)S(1)} %broadcast_compare_fusion.5, ...), kind=kOutput, calls=%fused_computation.30.clone.1 | convolution fusion | flops 144701440 | bytes 8273920 | tf_op jit(solution)/shard_map/transpose(jvp())/while/body/eval_jaxpr/checkpoint/hqk,khd->qhd/dot_general | solution.py:48
  162.9 1.9 fusion.189
  164.8 1.9 copy-done.2
  166.7 2.2 fusion.192
  168.9 4.6 %fusion.191 = bf16[1024,2,64]{0,2,1:T(8,128)(2,1)} fusion(bf16[2,64,512]{2,1,0:T(8,128)(2,1)S(1)} %bitcast.163, f32[2,512]{1,0:T(2,128)} %copy-done.9, f32[2,512,1024]{2,1,0:T(8,128)} %copy-done.1, f32[2,512]{1,0:T(2,128)} %copy-done.11, pred[512,1024]{1,0:T(8,128)(4,1)S(1)} %broadcast_compare_fusion.5, ...), kind=kOutput, calls=%fused_computation.52.clone.1 | convolution fusion | flops 139722752 | bytes 5382145 | tf_op jit(solution)/shard_map/transpose(jvp())/while/body/eval_jaxpr/checkpoint/hqk,khd->qhd/dot_general | solution.py:48
  173.5 3.2 %fusion.190 = bf16[1024,2,64]{0,2,1:T(8,128)(2,1)} fusion(bf16[512,2,64]{0,2,1:T(8,128)(2,1)S(1)} %dynamic-slice_bitcast_fusion.2, f32[2,512,1024]{2,1,0:T(8,128)S(1)} %copy-done.3, pred[2,512,1024]{2,1,0:T(32,128)(4,1)S(1)} %copy-done.22, f32[2,512]{1,0:T(2,128)S(1)} %copy-done.14, pred[512,1024]{1,0:T(8,128)(4,1)S(1)} %broadcast_compare_fusion.5, ...), kind=kOutput, calls=%fused_computation.53.clone.1 | convolution fusion | flops 138805248 | bytes 6426625 | tf_op jit(solution)/shard_map/transpose(jvp())/while/body/eval_jaxpr/checkpoint/qhd,khd->hqk/dot_general | solution.py:41
  176.7 1.3 copy.58
  178.7 1.7 convolution_bitcast_fusion.1
  181.1 1.3 pad_maximum_fusion
  182.4 21.8 %psum.15 = f32[]{:T(128)} all-reduce(f32[]{:T(128)} %get-tuple-element.442), channel_id=1, replica_groups=mesh['dp'=8,'mp'=4] {'dp'}, use_global_device_ids=true, to_apply=%region_26.27 | all-reduce | flops 1 | bytes 8 | tf_op jit(solution)/shard_map/psum | solution.py:142
  204.2 2.0 broadcast_divide_fusion.1
  206.2 57.0 %reduce-scatter.3.cloned.1.call-done = f32[128,3,128]{2,0,1:T(8,128)} async-done(((f32[1024,3,128]{2,0,1:T(8,128)}), f32[128,3,128]{2,0,1:T(8,128)}) %reduce-scatter.3.cloned.1.call-update) | async-done | bytes 196624 | tf_op jit(solution)/shard_map/reduce_scatter | solution.py:161
  263.3 2.2 broadcast_divide_fusion
  (144 shorter events, 24.4 us)
Async XLA Ops:
  7.2 32.9 %copy-start = (bf16[200,1024]{1,0:T(8,128)(2,1)S(1)}, bf16[200,1024]{1,0:T(8,128)(2,1)}, u32[]{:S(2)}) copy-start(bf16[200,1024]{1,0:T(8,128)(2,1)} %param.24) | copy-start | bytes 1228804
  11.4 15.4 %all-to-all-start = ((bf16[8,2,6400]{2,1,0:T(2,128)(2,1)}), bf16[8,2,6400]{2,1,0:T(2,128)(2,1)S(1)}, u32[]{:S(2)}, u32[]{:S(2)}) async-start(bf16[8,2,6400]{2,1,0:T(2,128)(2,1)} %reshape.344), calls=%async_computation | async-start | bytes 409600 | tf_op jit(solution)/shard_map/all_to_all | solution.py:103
  26.8 11.4 %all-to-all-start.1 = ((bf16[8,2,6400]{2,1,0:T(2,128)(2,1)}), bf16[8,2,6400]{2,1,0:T(2,128)(2,1)S(1)}, u32[]{:S(2)}, u32[]{:S(2)}) async-start(bf16[8,2,6400]{2,1,0:T(2,128)(2,1)} %reshape.342), calls=%async_computation.1 | async-start | bytes 409600 | tf_op jit(solution)/shard_map/all_to_all | solution.py:104
  30.4 85.8 %all-reduce.2.cloned.1.call-start = ((), (), s32[]{:S(2)}) async-start(), calls=%async_computation.4 | async-start | bytes 4194304 | tf_op jit(solution)/shard_map/psum | solution.py:134
  41.0 2.5 copy-start.4
  41.0 1.7 copy-start.16
  42.7 1.4 copy-start.5
  46.5 17.6 %copy-start.8 = (bf16[128,1024]{1,0:T(8,128)(2,1)S(1)}, bf16[128,1024]{1,0:T(8,128)(2,1)}, u32[]{:S(2)}) copy-start(bf16[128,1024]{1,0:T(8,128)(2,1)} %param.27) | copy-start | bytes 786436
  47.3 4.9 %copy-start.19 = (bf16[1024,2,64]{0,2,1:T(8,128)(2,1)S(1)}, bf16[1024,2,64]{0,2,1:T(8,128)(2,1)}, u32[]{:S(2)}) copy-start(bf16[1024,2,64]{0,2,1:T(8,128)(2,1)} %get-tuple-element.618) | copy-start | bytes 786436 | tf_op jit(solution)/shard_map/jvp()/while
  56.0 4.9 %copy-start.19 = (bf16[1024,2,64]{0,2,1:T(8,128)(2,1)S(1)}, bf16[1024,2,64]{0,2,1:T(8,128)(2,1)}, u32[]{:S(2)}) copy-start(bf16[1024,2,64]{0,2,1:T(8,128)(2,1)} %get-tuple-element.618) | copy-start | bytes 786436 | tf_op jit(solution)/shard_map/jvp()/while
  64.1 2.4 copy-start.17
  64.1 3.7 %copy-start.10 = (s32[1,1024]{1,0:T(1,128)}, s32[1,1024]{1,0:T(1,128)S(1)}, u32[]{:S(2)}) copy-start(s32[1,1024]{1,0:T(1,128)S(1)} %get-tuple-element.668) | copy-start | bytes 12292
  64.1 2.4 copy-start.15
  66.3 137.9 %reduce-scatter.5.cloned.1.call-start = ((), (), s32[]{:S(2)}) async-start(), calls=%async_computation.6 | async-start | bytes 589824 | tf_op jit(solution)/shard_map/reduce_scatter | solution.py:162
  119.8 5.2 %copy-start.7 = (bf16[1024,1024]{0,1:T(8,128)(2,1)}, bf16[1024,1024]{0,1:T(8,128)(2,1)S(1)}, u32[]{:S(2)}) copy-start(bf16[1024,1024]{0,1:T(8,128)(2,1)S(1)} %add_convert_fusion) | copy-start | bytes 6291460
  131.2 132.1 %reduce-scatter.3.cloned.1.call-start = ((), (), s32[]{:S(2)}) async-start(), calls=%async_computation.5 | async-start | bytes 1769472 | tf_op jit(solution)/shard_map/reduce_scatter | solution.py:161
  132.0 46.0 %copy-start.6 = (bf16[1024,1024]{0,1:T(8,128)(2,1)S(1)}, bf16[1024,1024]{0,1:T(8,128)(2,1)}, u32[]{:S(2)}) copy-start(bf16[1024,1024]{0,1:T(8,128)(2,1)} %copy-done.5) | copy-start | bytes 6291460
  134.9 3.3 %copy-start.20 = (bf16[1024,2,64]{0,2,1:T(8,128)(2,1)S(1)}, bf16[1024,2,64]{0,2,1:T(8,128)(2,1)}, u32[]{:S(2)}) copy-start(bf16[1024,2,64]{0,2,1:T(8,128)(2,1)} %get-tuple-element.589) | copy-start | bytes 786436 | tf_op jit(solution)/shard_map/transpose(jvp())/while
  137.0 4.0 %copy-start.1 = (f32[2,512,1024]{2,1,0:T(8,128)}, f32[2,512,1024]{2,1,0:T(8,128)S(1)}, u32[]{:S(2)}) copy-start(f32[2,512,1024]{2,1,0:T(8,128)S(1)} %get-tuple-element.587) | copy-start | bytes 12582916 | tf_op jit(solution)/shard_map/transpose(jvp())/while
  137.0 4.0 %copy-start.11 = (f32[2,512]{1,0:T(2,128)}, f32[2,512]{1,0:T(2,128)S(1)}, u32[]{:S(2)}) copy-start(f32[2,512]{1,0:T(2,128)S(1)} %get-tuple-element.586) | copy-start | bytes 12292 | tf_op jit(solution)/shard_map/transpose(jvp())/while
  138.2 2.9 %copy-start.9 = (f32[2,512]{1,0:T(2,128)}, f32[2,512]{1,0:T(2,128)S(1)}, u32[]{:S(2)}) copy-start(f32[2,512]{1,0:T(2,128)S(1)} %fusion.188) | copy-start | bytes 12292 | tf_op jit(solution)/shard_map/transpose(jvp())/while
  141.0 2.0 copy-start.21
  141.0 3.9 %copy-start.18 = (bf16[1024,2,64]{0,2,1:T(8,128)(2,1)S(1)}, bf16[1024,2,64]{0,2,1:T(8,128)(2,1)}, u32[]{:S(2)}) copy-start(bf16[1024,2,64]{0,2,1:T(8,128)(2,1)} %get-tuple-element.585) | copy-start | bytes 786436 | tf_op jit(solution)/shard_map/transpose(jvp())/while
  143.0 2.0 copy-start.2
  143.0 1.9 copy-start.13
  147.1 4.5 %copy-start.3 = (f32[2,512,1024]{2,1,0:T(8,128)S(1)}, f32[2,512,1024]{2,1,0:T(8,128)}, u32[]{:S(2)}) copy-start(f32[2,512,1024]{2,1,0:T(8,128)} %copy-done.2) | copy-start | bytes 12582916 | tf_op jit(solution)/shard_map/transpose(jvp())/while
  147.1 4.5 %copy-start.14 = (f32[2,512]{1,0:T(2,128)S(1)}, f32[2,512]{1,0:T(2,128)}, u32[]{:S(2)}) copy-start(f32[2,512]{1,0:T(2,128)} %copy-done.13) | copy-start | bytes 12292 | tf_op jit(solution)/shard_map/transpose(jvp())/while
  147.1 4.5 %copy-start.22 = (pred[2,512,1024]{2,1,0:T(32,128)(4,1)S(1)}, pred[2,512,1024]{2,1,0:T(32,128)(4,1)}, u32[]{:S(2)}) copy-start(pred[2,512,1024]{2,1,0:T(32,128)(4,1)} %copy-done.21) | copy-start | bytes 3145732 | tf_op jit(solution)/shard_map/transpose(jvp())/while
  156.7 3.3 %copy-start.20 = (bf16[1024,2,64]{0,2,1:T(8,128)(2,1)S(1)}, bf16[1024,2,64]{0,2,1:T(8,128)(2,1)}, u32[]{:S(2)}) copy-start(bf16[1024,2,64]{0,2,1:T(8,128)(2,1)} %get-tuple-element.589) | copy-start | bytes 786436 | tf_op jit(solution)/shard_map/transpose(jvp())/while
  158.8 4.0 %copy-start.1 = (f32[2,512,1024]{2,1,0:T(8,128)}, f32[2,512,1024]{2,1,0:T(8,128)S(1)}, u32[]{:S(2)}) copy-start(f32[2,512,1024]{2,1,0:T(8,128)S(1)} %get-tuple-element.587) | copy-start | bytes 12582916 | tf_op jit(solution)/shard_map/transpose(jvp())/while
  158.8 4.0 %copy-start.11 = (f32[2,512]{1,0:T(2,128)}, f32[2,512]{1,0:T(2,128)S(1)}, u32[]{:S(2)}) copy-start(f32[2,512]{1,0:T(2,128)S(1)} %get-tuple-element.586) | copy-start | bytes 12292 | tf_op jit(solution)/shard_map/transpose(jvp())/while
  160.0 2.9 %copy-start.9 = (f32[2,512]{1,0:T(2,128)}, f32[2,512]{1,0:T(2,128)S(1)}, u32[]{:S(2)}) copy-start(f32[2,512]{1,0:T(2,128)S(1)} %fusion.188) | copy-start | bytes 12292 | tf_op jit(solution)/shard_map/transpose(jvp())/while
  162.8 2.0 copy-start.21
  162.8 3.9 %copy-start.18 = (bf16[1024,2,64]{0,2,1:T(8,128)(2,1)S(1)}, bf16[1024,2,64]{0,2,1:T(8,128)(2,1)}, u32[]{:S(2)}) copy-start(bf16[1024,2,64]{0,2,1:T(8,128)(2,1)} %get-tuple-element.585) | copy-start | bytes 786436 | tf_op jit(solution)/shard_map/transpose(jvp())/while
  164.8 2.0 copy-start.2
  164.8 1.9 copy-start.13
  168.9 4.6 %copy-start.3 = (f32[2,512,1024]{2,1,0:T(8,128)S(1)}, f32[2,512,1024]{2,1,0:T(8,128)}, u32[]{:S(2)}) copy-start(f32[2,512,1024]{2,1,0:T(8,128)} %copy-done.2) | copy-start | bytes 12582916 | tf_op jit(solution)/shard_map/transpose(jvp())/while
  168.9 4.6 %copy-start.14 = (f32[2,512]{1,0:T(2,128)S(1)}, f32[2,512]{1,0:T(2,128)}, u32[]{:S(2)}) copy-start(f32[2,512]{1,0:T(2,128)} %copy-done.13) | copy-start | bytes 12292 | tf_op jit(solution)/shard_map/transpose(jvp())/while
  168.9 4.6 %copy-start.22 = (pred[2,512,1024]{2,1,0:T(32,128)(4,1)S(1)}, pred[2,512,1024]{2,1,0:T(32,128)(4,1)}, u32[]{:S(2)}) copy-start(pred[2,512,1024]{2,1,0:T(32,128)(4,1)} %copy-done.21) | copy-start | bytes 3145732 | tf_op jit(solution)/shard_map/transpose(jvp())/while
  176.7 3.7 %copy-start.12 = (bf16[1024,2,64]{0,2,1:T(8,128)(2,1)S(1)}, bf16[1024,2,64]{0,2,1:T(8,128)(2,1)}, u32[]{:S(2)}) copy-start(bf16[1024,2,64]{0,2,1:T(8,128)(2,1)} %get-tuple-element.274) | copy-start | bytes 786436
Sparse Core Ops, SparseCore 0:
  66.4 49.7 all-reduce.1
  131.3 63.3 reduce-scatter.4
  198.2 65.0 reduce-scatter.2
where the time goes:
time: 273 us; the launch traced here: 272 us
  waiting for transfers between devices  113 us (41%)
  matrix products  62 us (23%)
  other arithmetic  29 us (11%)
  blocking collectives  21.8 us (8%)
  local copies, waits for them, and re-layouts  20.8 us (8%)
  between operations  14.1 us (5%)
  starting transfers between devices  11.2 us (4%)
    reduce_scatter x1, waiting for transfers between devices, shards(): lax.psum_scatter(qkv_terms, 'dp', scatter_dimension=0, tiled=True)  57 us
    psum x1, waiting for transfers between devices, shards(): mixed = lax.psum(partial_mix.astype(jnp.bfloat16), 'mp').astype(jnp.float32)  48.4 us
    psum x1, blocking collectives, shards(): count = lax.psum(jnp.sum(masked), 'dp')  21.8 us
    dot_general x6, matrix products, one_block(): jnp.einsum('hqk,khd->qhd', probs, valued, preferred_element_type=jnp.floa...  20.7 us
    dot_general x6, matrix products, one_block(): jnp.einsum('qhd,khd->hqk', query_block, keyed, preferred_element_type=jnp...  14 us
    sub x2, matrix products, one_block(): weights = jnp.exp(scores - top)  9.01 us
    all_to_all x1, starting transfers between devices, shards(): lax.all_to_all(outgoing(noise_blocks), 'dp', split_axis=0, concat_axis=0,...  7.31 us
  transfers between devices with their start and end apart: 5, of which 4 were waited for; matrix products, arithmetic and copies ran while one was open for 22% of the time, Pallas kernels for 0%

commit v1 on v0

--- a/solution.py
+++ b/solution.py
@@ -131,7 +131,9 @@
     heads_out, pullback = jax.vjp(lambda a, b, c: attend(a, b, c, segment), query, keys, values)
     attended = heads_out.astype(jnp.bfloat16)
     partial_mix = jnp.dot(attended, out_proj, preferred_element_type=jnp.float32)
-    mixed = lax.psum(partial_mix.astype(jnp.bfloat16), "mp").astype(jnp.float32)
+    mixed = jnp.sum(lax.all_gather(partial_mix.astype(jnp.bfloat16), "mp"), axis=0).astype(
+        jnp.float32
+    )
     hidden1 = (hidden0 + mixed).astype(jnp.bfloat16)
     wide1 = lax.optimization_barrier(hidden1).astype(jnp.float32)
     rscale = lax.rsqrt(jnp.mean(wide1 * wide1, axis=1, keepdims=True) + 1e-06)

time: 273 us -> 289 us (1.059)
  other arithmetic: 29 us -> 35.6 us
  waiting for transfers between devices: 113 us -> 119 us
    all_gather x0 -> x1, waiting for transfers between devices: none -> 55.3 us  [shards(): lax.all_gather(partial_mix.astype(jnp.bfloat16), 'mp')]
    psum x1 -> x0, waiting for transfers between devices: 48.4 us -> none  [shards(): mixed = lax.psum(partial_mix.astype(jnp.bfloat16), 'mp').astype(jnp.float32)]
    reduce_sum x0 -> x1, other arithmetic: none -> 6.5 us  [shards(): jnp.sum(lax.all_gather(partial_mix.astype(jnp.bfloat16), 'mp'), axis=0)]
  transfers between devices with their start and end apart: 5 -> 5, of which waited for: 4 -> 4; matrix products, arithmetic and copies ran while one was open for 22% -> 20% of each run, Pallas kernels for 0% -> 0%
where the time goes in v1:
time: 289 us; the launch traced here: 288 us
  waiting for transfers between devices  119 us (41%)
  matrix products  61.8 us (21%)
  other arithmetic  35.6 us (12%)
  local copies, waits for them, and re-layouts  23.3 us (8%)
  blocking collectives  21.9 us (8%)
  between operations  14.1 us (5%)
  starting transfers between devices  11.4 us (4%)
    reduce_scatter x1, waiting for transfers between devices, shards(): lax.psum_scatter(qkv_terms, 'dp', scatter_dimension=0, tiled=True)  56.7 us
    all_gather x1, waiting for transfers between devices, shards(): lax.all_gather(partial_mix.astype(jnp.bfloat16), 'mp')  55.3 us
    psum x1, blocking collectives, shards(): count = lax.psum(jnp.sum(masked), 'dp')  21.9 us
    dot_general x6, matrix products, one_block(): jnp.einsum('hqk,khd->qhd', probs, valued, preferred_element_type=jnp.floa...  20.6 us
    dot_general x6, matrix products, one_block(): jnp.einsum('qhd,khd->hqk', query_block, keyed, preferred_element_type=jnp...  13.9 us
    sub x2, matrix products, one_block(): weights = jnp.exp(scores - top)  8.92 us
    all_to_all x1, starting transfers between devices, shards(): lax.all_to_all(outgoing(noise_blocks), 'dp', split_axis=0, concat_axis=0,...  7.31 us
    reduce_sum x1, other arithmetic, shards(): jnp.sum(lax.all_gather(partial_mix.astype(jnp.bfloat16), 'mp'), axis=0)  6.5 us
  transfers between devices with their start and end apart: 5, of which 4 were waited for; matrix products, arithmetic and copies ran while one was open for 20% of the time, Pallas kernels for 0%

profile of v1, /device:TPU:0, one launch (start us, length us, event | category | flops | bytes accessed | tf_op | source)
XLA Modules:
  0.0 287.8 jit_solution(14268232974094928721)
XLA Ops:
  8.3 1.1 fusion.60
  11.4 7.3 %all-to-all-start = ((bf16[8,2,6400]{2,1,0:T(2,128)(2,1)}), bf16[8,2,6400]{2,1,0:T(2,128)(2,1)S(1)}, u32[]{:S(2)}, u32[]{:S(2)}) async-start(bf16[8,2,6400]{2,1,0:T(2,128)(2,1)} %reshape.345), calls=%async_computation | async-start | bytes 409600 | tf_op jit(solution)/shard_map/all_to_all | solution.py:103
  21.7 1.1 fusion.61
  24.4 2.4 all-to-all-done
  26.8 3.6 %all-to-all-start.1 = ((bf16[8,2,6400]{2,1,0:T(2,128)(2,1)}), bf16[8,2,6400]{2,1,0:T(2,128)(2,1)S(1)}, u32[]{:S(2)}, u32[]{:S(2)}) async-start(bf16[8,2,6400]{2,1,0:T(2,128)(2,1)} %reshape.343), calls=%async_computation.1 | async-start | bytes 409600 | tf_op jit(solution)/shard_map/all_to_all | solution.py:104
  33.4 4.8 %all-to-all-done.1 = bf16[8,2,6400]{2,1,0:T(2,128)(2,1)S(1)} async-done(((bf16[8,2,6400]{2,1,0:T(2,128)(2,1)}), bf16[8,2,6400]{2,1,0:T(2,128)(2,1)S(1)}, u32[]{:S(2)}, u32[]{:S(2)}) %all-to-all-start.1) | async-done | bytes 204832 | tf_op jit(solution)/shard_map/all_to_all | solution.py:104
  41.4 1.3 copy-done.16
  44.0 1.2 convolution_convert_fusion.7
  46.5 17.5 %while.30 = (s32[]{:T(128)}, bf16[2,512,128]{2,1,0:T(8,128)(2,1)S(1)}, s32[2,512]{1,0:T(2,128)}, s32[1,1024]{1,0:T(1,128)S(1)}, bf16[2,512,2,64]{1,3,2,0:T(8,128...) while((s32[]{:T(128)}, bf16[2,512,128]{2,1,0:T(8,128)(2,1)S(1)}, ...), condition=%wide.region_13.14_spmd, body=%wide.region_10.13_spmd.sunk | while | flops 275252224 | bytes 11815545 | solution.py:52
  47.6 4.5 %fusion.178 = (f32[2,512]{1,0:T(2,128)S(1)}, f32[2,512,1024]{2,1,0:T(8,128)}) fusion(pred[512,1024]{1,0:T(8,128)(4,1)S(1)} %broadcast_compare_fusion.4, bf16[1024,2,64]{0,2,1:T(8,128)(2,1)S(1)} %get-tuple-element.617, bf16[2,512,2,64]{1,3,2,0:T(8,128)(2,1)} %get-tuple-element.616, s32[]{:T(128)} %get-tuple-element.604), kind=kOutput, calls=%fused_computation.176.clone.1 | convolution fusion | flops 138413056 | bytes 5116416 | tf_op jit(solution)/shard_map/jvp()/while/body/eval_jaxpr/sub | solution.py:46
  52.1 3.0 %fusion.179 = bf16[2,512,64]{1,2,0:T(8,128)(2,1)S(1)} fusion(bf16[1024,2,64]{0,2,1:T(8,128)(2,1)S(1)} %copy-done.19, f32[2,512,1024]{2,1,0:T(8,128)} %get-tuple-element.570, f32[2,512]{1,0:T(2,128)S(1)} %get-tuple-element.571), kind=kOutput, calls=%fused_computation.8.clone.1 | convolution fusion | flops 136314880 | bytes 4591616 | tf_op jit(solution)/shard_map/jvp()/while/body/eval_jaxpr/hqk,khd->qhd/dot_general | solution.py:48
  56.3 4.5 %fusion.178 = (f32[2,512]{1,0:T(2,128)S(1)}, f32[2,512,1024]{2,1,0:T(8,128)}) fusion(pred[512,1024]{1,0:T(8,128)(4,1)S(1)} %broadcast_compare_fusion.4, bf16[1024,2,64]{0,2,1:T(8,128)(2,1)S(1)} %get-tuple-element.617, bf16[2,512,2,64]{1,3,2,0:T(8,128)(2,1)} %get-tuple-element.616, s32[]{:T(128)} %get-tuple-element.604), kind=kOutput, calls=%fused_computation.176.clone.1 | convolution fusion | flops 138413056 | bytes 5116416 | tf_op jit(solution)/shard_map/jvp()/while/body/eval_jaxpr/sub | solution.py:46
  60.8 3.0 %fusion.179 = bf16[2,512,64]{1,2,0:T(8,128)(2,1)S(1)} fusion(bf16[1024,2,64]{0,2,1:T(8,128)(2,1)S(1)} %copy-done.19, f32[2,512,1024]{2,1,0:T(8,128)} %get-tuple-element.570, f32[2,512]{1,0:T(2,128)S(1)} %get-tuple-element.571), kind=kOutput, calls=%fused_computation.8.clone.1 | convolution fusion | flops 136314880 | bytes 4591616 | tf_op jit(solution)/shard_map/jvp()/while/body/eval_jaxpr/hqk,khd->qhd/dot_general | solution.py:48
  64.0 2.0 convolution_convert_fusion.5
  67.6 55.3 %all-gather.3.cloned.1.call-done = bf16[4096,1024]{1,0:T(8,128)(2,1)} async-done(((bf16[1024,1024]{1,0:T(8,128)(2,1)}), bf16[4096,1024]{1,0:T(8,128)(2,1)}) %all-gather.3.cloned.1.call-update) | async-done | bytes 8388624 | tf_op jit(solution)/shard_map/all_gather | solution.py:134
  122.8 6.5 %reduce_sum.208 = bf16[1024,1024]{1,0:T(8,128)(2,1)S(1)} reduce(bf16[4,1024,1024]{2,1,0:T(8,128)(2,1)} %bitcast.162, bf16[]{:T(256)} %constant.183.clone.1), dimensions={0}, to_apply=%region_14.15 | reduce | flops 3145728 | bytes 10485762 | tf_op jit(solution)/shard_map/reduce_sum | solution.py:134
  129.3 2.6 copy.51
  131.9 3.6 %add_convert_fusion = bf16[1024,1024]{0,1:T(8,128)(2,1)S(1)} fusion(f32[1024,1024]{0,1:T(8,128)} %copy-done.4, bf16[1024,1024]{0,1:T(8,128)(2,1)} %copy.51), kind=kLoop, calls=%fused_computation.88 | loop fusion | flops 3145728 | bytes 8388608 | tf_op jit(solution)/shard_map/convert_element_type | solution.py:137
  136.1 4.7 %fusion.66 = (f32[1024]{0:T(1024)S(1)}, f32[1024,1024]{0,1:T(8,128)}) fusion(bf16[1024,1024]{0,1:T(8,128)(2,1)S(1)} %add_convert_fusion, f32[1024]{0:T(1024)S(1)} %convert_element_type.202, f32[1024]{0:T(1024)S(1)} %add_rsqrt_fusion, bf16[1024,100]{0,1:T(8,128)(2,1)} %param.29, f32[1024,100]{0,1:T(8,128)} %copy.52, f32[1024,100]{0,1:T(8,128)S(1)} %copy.53, ...), kind=kOutput, calls=%fused_computation.83 | convolution fusion | flops 429276160 | bytes 7331840 | tf_op jit(solution)/shard_map/dot_general | solution.py:146
  140.8 3.7 %fusion.69 = bf16[1024,1024]{0,1:T(8,128)(2,1)S(1)} fusion(bf16[1024,1024]{0,1:T(8,128)(2,1)} %copy-done.7, f32[1024,1024]{0,1:T(8,128)} %get-tuple-element.459, f32[1024]{0:T(1024)S(1)} %broadcast_multiply_fusion, f32[1024]{0:T(1024)S(1)} %convert_element_type.202, f32[1024]{0:T(1024)S(1)} %add_rsqrt_fusion), kind=kLoop, calls=%fused_computation.86 | loop fusion | flops 7340032 | bytes 8400896 | tf_op jit(solution)/shard_map/convert_element_type | solution.py:150
  144.5 1.6 fusion.126
  148.0 44.7 %while.31 = (s32[]{:T(128)}, bf16[1024,2,64]{0,2,1:T(8,128)(2,1)}, bf16[1024,2,64]{0,2,1:T(8,128)(2,1)}, bf16[2,512,2,64]{1,3,2,0:T(8,128)(2,1)}, bf16[2,512,2,6...) while((s32[]{:T(128)}, bf16[1024,2,64]{0,2,1:T(8,128)(2,1)}, ...), condition=%wide.region_23.24_spmd.clone, body=%wide.region_17.23_spmd.clone.sunk | while | flops 712179712 | bytes 109349352 | solution.py:52
  148.1 1.0 dynamic-slice_bitcast_fusion.2
  149.8 1.0 broadcast_compare_fusion.5
  150.9 2.1 fusion.187
  153.0 1.2 fusion.188
  154.2 2.8 convert_reduce_fusion.5
  157.0 1.9 fusion.189
  159.0 1.9 copy-done.2
  160.9 2.2 fusion.192
  163.1 4.5 %fusion.191 = bf16[1024,2,64]{0,2,1:T(8,128)(2,1)} fusion(bf16[2,64,512]{2,1,0:T(8,128)(2,1)S(1)} %bitcast.165, f32[2,512]{1,0:T(2,128)} %copy-done.9, f32[2,512,1024]{2,1,0:T(8,128)} %copy-done.1, f32[2,512]{1,0:T(2,128)} %copy-done.11, pred[512,1024]{1,0:T(8,128)(4,1)S(1)} %broadcast_compare_fusion.5, ...), kind=kOutput, calls=%fused_computation.52.clone.1 | convolution fusion | flops 139722752 | bytes 5382145 | tf_op jit(solution)/shard_map/transpose(jvp())/while/body/eval_jaxpr/checkpoint/hqk,khd->qhd/dot_general | solution.py:48
  167.6 2.3 fusion.190
  171.6 1.0 broadcast_compare_fusion.5
  172.7 2.1 fusion.187
  174.8 1.2 fusion.188
  176.0 2.8 convert_reduce_fusion.5
  178.8 1.9 fusion.189
  180.8 1.9 copy-done.2
  182.7 2.1 fusion.192
  184.9 4.5 %fusion.191 = bf16[1024,2,64]{0,2,1:T(8,128)(2,1)} fusion(bf16[2,64,512]{2,1,0:T(8,128)(2,1)S(1)} %bitcast.165, f32[2,512]{1,0:T(2,128)} %copy-done.9, f32[2,512,1024]{2,1,0:T(8,128)} %copy-done.1, f32[2,512]{1,0:T(2,128)} %copy-done.11, pred[512,1024]{1,0:T(8,128)(4,1)S(1)} %broadcast_compare_fusion.5, ...), kind=kOutput, calls=%fused_computation.52.clone.1 | convolution fusion | flops 139722752 | bytes 5382145 | tf_op jit(solution)/shard_map/transpose(jvp())/while/body/eval_jaxpr/checkpoint/hqk,khd->qhd/dot_general | solution.py:48
  189.4 3.2 %fusion.190 = bf16[1024,2,64]{0,2,1:T(8,128)(2,1)} fusion(bf16[512,2,64]{0,2,1:T(8,128)(2,1)S(1)} %dynamic-slice_bitcast_fusion.2, f32[2,512,1024]{2,1,0:T(8,128)S(1)} %copy-done.3, pred[2,512,1024]{2,1,0:T(32,128)(4,1)S(1)} %copy-done.22, f32[2,512]{1,0:T(2,128)S(1)} %copy-done.14, pred[512,1024]{1,0:T(8,128)(4,1)S(1)} %broadcast_compare_fusion.5, ...), kind=kOutput, calls=%fused_computation.53.clone.1 | convolution fusion | flops 138805248 | bytes 6426625 | tf_op jit(solution)/shard_map/transpose(jvp())/while/body/eval_jaxpr/checkpoint/qhd,khd->hqk/dot_general | solution.py:41
  192.6 1.3 copy.56
  194.6 1.7 convolution_bitcast_fusion.1
  197.0 1.3 pad_maximum_fusion
  198.3 21.9 %psum.7 = f32[]{:T(128)} all-reduce(f32[]{:T(128)} %get-tuple-element.442), channel_id=1, replica_groups=mesh['dp'=8,'mp'=4] {'dp'}, use_global_device_ids=true, to_apply=%region_26.27 | all-reduce | flops 1 | bytes 8 | tf_op jit(solution)/shard_map/psum | solution.py:144
  220.2 2.1 broadcast_divide_fusion.1
  222.3 56.7 %reduce-scatter.3.cloned.1.call-done = f32[128,3,128]{2,0,1:T(8,128)} async-done(((f32[1024,3,128]{2,0,1:T(8,128)}), f32[128,3,128]{2,0,1:T(8,128)}) %reduce-scatter.3.cloned.1.call-update) | async-done | bytes 196624 | tf_op jit(solution)/shard_map/reduce_scatter | solution.py:163
  279.0 2.2 broadcast_divide_fusion
  (146 shorter events, 26.6 us)
Async XLA Ops:
  7.2 32.9 %copy-start = (bf16[200,1024]{1,0:T(8,128)(2,1)S(1)}, bf16[200,1024]{1,0:T(8,128)(2,1)}, u32[]{:S(2)}) copy-start(bf16[200,1024]{1,0:T(8,128)(2,1)} %param.24) | copy-start | bytes 1228804
  11.4 15.4 %all-to-all-start = ((bf16[8,2,6400]{2,1,0:T(2,128)(2,1)}), bf16[8,2,6400]{2,1,0:T(2,128)(2,1)S(1)}, u32[]{:S(2)}, u32[]{:S(2)}) async-start(bf16[8,2,6400]{2,1,0:T(2,128)(2,1)} %reshape.345), calls=%async_computation | async-start | bytes 409600 | tf_op jit(solution)/shard_map/all_to_all | solution.py:103
  26.8 11.4 %all-to-all-start.1 = ((bf16[8,2,6400]{2,1,0:T(2,128)(2,1)}), bf16[8,2,6400]{2,1,0:T(2,128)(2,1)S(1)}, u32[]{:S(2)}, u32[]{:S(2)}) async-start(bf16[8,2,6400]{2,1,0:T(2,128)(2,1)} %reshape.343), calls=%async_computation.1 | async-start | bytes 409600 | tf_op jit(solution)/shard_map/all_to_all | solution.py:104
  30.4 92.5 %all-gather.3.cloned.1.call-start = ((), (), s32[]{:S(2)}) async-start(), calls=%async_computation.6 | async-start | bytes 10485760 | tf_op jit(solution)/shard_map/all_gather | solution.py:134
  40.9 2.5 copy-start.4
  41.0 1.7 copy-start.16
  42.7 1.4 copy-start.5
  46.5 17.5 %copy-start.8 = (bf16[128,1024]{1,0:T(8,128)(2,1)S(1)}, bf16[128,1024]{1,0:T(8,128)(2,1)}, u32[]{:S(2)}) copy-start(bf16[128,1024]{1,0:T(8,128)(2,1)} %param.27) | copy-start | bytes 786436
  47.2 4.8 %copy-start.19 = (bf16[1024,2,64]{0,2,1:T(8,128)(2,1)S(1)}, bf16[1024,2,64]{0,2,1:T(8,128)(2,1)}, u32[]{:S(2)}) copy-start(bf16[1024,2,64]{0,2,1:T(8,128)(2,1)} %get-tuple-element.618) | copy-start | bytes 786436 | tf_op jit(solution)/shard_map/jvp()/while
  56.0 4.8 %copy-start.19 = (bf16[1024,2,64]{0,2,1:T(8,128)(2,1)S(1)}, bf16[1024,2,64]{0,2,1:T(8,128)(2,1)}, u32[]{:S(2)}) copy-start(bf16[1024,2,64]{0,2,1:T(8,128)(2,1)} %get-tuple-element.618) | copy-start | bytes 786436 | tf_op jit(solution)/shard_map/jvp()/while
  64.0 2.3 copy-start.17
  64.0 58.8 %copy-start.10 = (s32[1,1024]{1,0:T(1,128)}, s32[1,1024]{1,0:T(1,128)S(1)}, u32[]{:S(2)}) copy-start(s32[1,1024]{1,0:T(1,128)S(1)} %get-tuple-element.668) | copy-start | bytes 12292
  64.0 2.3 copy-start.15
  66.1 154.2 %reduce-scatter.5.cloned.1.call-start = ((), (), s32[]{:S(2)}) async-start(), calls=%async_computation.5 | async-start | bytes 589824 | tf_op jit(solution)/shard_map/reduce_scatter | solution.py:164
  135.6 5.2 %copy-start.7 = (bf16[1024,1024]{0,1:T(8,128)(2,1)}, bf16[1024,1024]{0,1:T(8,128)(2,1)S(1)}, u32[]{:S(2)}) copy-start(bf16[1024,1024]{0,1:T(8,128)(2,1)S(1)} %add_convert_fusion) | copy-start | bytes 6291460
  147.0 132.0 %reduce-scatter.3.cloned.1.call-start = ((), (), s32[]{:S(2)}) async-start(), calls=%async_computation.4 | async-start | bytes 1769472 | tf_op jit(solution)/shard_map/reduce_scatter | solution.py:163
  148.0 46.0 %copy-start.6 = (bf16[1024,1024]{0,1:T(8,128)(2,1)S(1)}, bf16[1024,1024]{0,1:T(8,128)(2,1)}, u32[]{:S(2)}) copy-start(bf16[1024,1024]{0,1:T(8,128)(2,1)} %copy-done.5) | copy-start | bytes 6291460
  150.9 3.3 %copy-start.20 = (bf16[1024,2,64]{0,2,1:T(8,128)(2,1)S(1)}, bf16[1024,2,64]{0,2,1:T(8,128)(2,1)}, u32[]{:S(2)}) copy-start(bf16[1024,2,64]{0,2,1:T(8,128)(2,1)} %get-tuple-element.589) | copy-start | bytes 786436 | tf_op jit(solution)/shard_map/transpose(jvp())/while
  153.0 4.0 %copy-start.1 = (f32[2,512,1024]{2,1,0:T(8,128)}, f32[2,512,1024]{2,1,0:T(8,128)S(1)}, u32[]{:S(2)}) copy-start(f32[2,512,1024]{2,1,0:T(8,128)S(1)} %get-tuple-element.587) | copy-start | bytes 12582916 | tf_op jit(solution)/shard_map/transpose(jvp())/while
  153.0 4.0 %copy-start.11 = (f32[2,512]{1,0:T(2,128)}, f32[2,512]{1,0:T(2,128)S(1)}, u32[]{:S(2)}) copy-start(f32[2,512]{1,0:T(2,128)S(1)} %get-tuple-element.586) | copy-start | bytes 12292 | tf_op jit(solution)/shard_map/transpose(jvp())/while
  154.2 2.9 copy-start.9
  157.0 2.0 copy-start.21
  157.0 3.9 %copy-start.18 = (bf16[1024,2,64]{0,2,1:T(8,128)(2,1)S(1)}, bf16[1024,2,64]{0,2,1:T(8,128)(2,1)}, u32[]{:S(2)}) copy-start(bf16[1024,2,64]{0,2,1:T(8,128)(2,1)} %get-tuple-element.585) | copy-start | bytes 786436 | tf_op jit(solution)/shard_map/transpose(jvp())/while
  158.9 2.0 copy-start.2
  159.0 1.9 copy-start.13
  163.1 4.5 %copy-start.3 = (f32[2,512,1024]{2,1,0:T(8,128)S(1)}, f32[2,512,1024]{2,1,0:T(8,128)}, u32[]{:S(2)}) copy-start(f32[2,512,1024]{2,1,0:T(8,128)} %copy-done.2) | copy-start | bytes 12582916 | tf_op jit(solution)/shard_map/transpose(jvp())/while
  163.1 4.5 %copy-start.14 = (f32[2,512]{1,0:T(2,128)S(1)}, f32[2,512]{1,0:T(2,128)}, u32[]{:S(2)}) copy-start(f32[2,512]{1,0:T(2,128)} %copy-done.13) | copy-start | bytes 12292 | tf_op jit(solution)/shard_map/transpose(jvp())/while
  163.1 4.5 %copy-start.22 = (pred[2,512,1024]{2,1,0:T(32,128)(4,1)S(1)}, pred[2,512,1024]{2,1,0:T(32,128)(4,1)}, u32[]{:S(2)}) copy-start(pred[2,512,1024]{2,1,0:T(32,128)(4,1)} %copy-done.21) | copy-start | bytes 3145732 | tf_op jit(solution)/shard_map/transpose(jvp())/while
  172.7 3.3 %copy-start.20 = (bf16[1024,2,64]{0,2,1:T(8,128)(2,1)S(1)}, bf16[1024,2,64]{0,2,1:T(8,128)(2,1)}, u32[]{:S(2)}) copy-start(bf16[1024,2,64]{0,2,1:T(8,128)(2,1)} %get-tuple-element.589) | copy-start | bytes 786436 | tf_op jit(solution)/shard_map/transpose(jvp())/while
  174.8 4.0 %copy-start.1 = (f32[2,512,1024]{2,1,0:T(8,128)}, f32[2,512,1024]{2,1,0:T(8,128)S(1)}, u32[]{:S(2)}) copy-start(f32[2,512,1024]{2,1,0:T(8,128)S(1)} %get-tuple-element.587) | copy-start | bytes 12582916 | tf_op jit(solution)/shard_map/transpose(jvp())/while
  174.8 4.0 %copy-start.11 = (f32[2,512]{1,0:T(2,128)}, f32[2,512]{1,0:T(2,128)S(1)}, u32[]{:S(2)}) copy-start(f32[2,512]{1,0:T(2,128)S(1)} %get-tuple-element.586) | copy-start | bytes 12292 | tf_op jit(solution)/shard_map/transpose(jvp())/while
  175.9 2.9 copy-start.9
  178.8 2.0 copy-start.21
  178.8 3.9 %copy-start.18 = (bf16[1024,2,64]{0,2,1:T(8,128)(2,1)S(1)}, bf16[1024,2,64]{0,2,1:T(8,128)(2,1)}, u32[]{:S(2)}) copy-start(bf16[1024,2,64]{0,2,1:T(8,128)(2,1)} %get-tuple-element.585) | copy-start | bytes 786436 | tf_op jit(solution)/shard_map/transpose(jvp())/while
  180.7 2.0 copy-start.2
  180.8 1.9 copy-start.13
  184.9 4.5 %copy-start.3 = (f32[2,512,1024]{2,1,0:T(8,128)S(1)}, f32[2,512,1024]{2,1,0:T(8,128)}, u32[]{:S(2)}) copy-start(f32[2,512,1024]{2,1,0:T(8,128)} %copy-done.2) | copy-start | bytes 12582916 | tf_op jit(solution)/shard_map/transpose(jvp())/while
  184.9 4.5 %copy-start.14 = (f32[2,512]{1,0:T(2,128)S(1)}, f32[2,512]{1,0:T(2,128)}, u32[]{:S(2)}) copy-start(f32[2,512]{1,0:T(2,128)} %copy-done.13) | copy-start | bytes 12292 | tf_op jit(solution)/shard_map/transpose(jvp())/while
  184.9 4.5 %copy-start.22 = (pred[2,512,1024]{2,1,0:T(32,128)(4,1)S(1)}, pred[2,512,1024]{2,1,0:T(32,128)(4,1)}, u32[]{:S(2)}) copy-start(pred[2,512,1024]{2,1,0:T(32,128)(4,1)} %copy-done.21) | copy-start | bytes 3145732 | tf_op jit(solution)/shard_map/transpose(jvp())/while
  192.6 3.7 %copy-start.12 = (bf16[1024,2,64]{0,2,1:T(8,128)(2,1)S(1)}, bf16[1024,2,64]{0,2,1:T(8,128)(2,1)}, u32[]{:S(2)}) copy-start(bf16[1024,2,64]{0,2,1:T(8,128)(2,1)} %get-tuple-element.274) | copy-start | bytes 786436
Sparse Core Ops, SparseCore 0:
  66.2 56.5 all-gather.2
  147.1 63.2 reduce-scatter.4
  213.8 65.1 reduce-scatter.2
